TPU v7x, 32 devices: a whole 2x2x4 slice. The times are simulated.
32 devices in a mesh: south: 4 (over y, x), east: 4 (over z), down: 2 (over core).
Axes of the slice: x: 2, y: 2, z: 4, core: 2. Of those that a mesh axis runs over, the one named last changes fastest.
Arguments:
- field_values: float32 [32, 384, 16, 128], P('south', 'east', 'down'), may hold values from 0.2 to 1.8
- flow_y: float32 [32, 384, 16, 128], P('south', 'east', 'down'), may hold values from -0.3 to 0.3
- flow_x: float32 [32, 384, 16, 128], P('south', 'east', 'down'), may hold values from -0.3 to 0.3
- flow_z: float32 [32, 384, 16, 128], P('south', 'east', 'down'), may hold values from -0.3 to 0.3
Outputs:
- potential: float32 [32, 384, 16, 128], P('south', 'east', 'down')
- field_values_end: float32 [32, 384, 16, 128], P('south', 'east', 'down')
All inputs are finite; a program needn't handle non-finite values.
Results may differ from a plain program's by a relative error of at most 0.00002.
Values sent between devices are 32-bit elements; how exact they have to be, the bound alone decides.
A program may use at most 128 MiB of HBM per device.

v0:
```python
import jax
import jax.numpy as jnp
from jax import lax
from jax.sharding import PartitionSpec as P

STEPS = 4


def extended(array, sides, width):
    for axis, dim in sides:
        size, length = (lax.axis_size(axis), array.shape[dim])
        up = [(i, (i + 1) % size) for i in range(size)]
        down = [(j, i) for i, j in up]
        last = lax.slice_in_dim(array, length - width, length, axis=dim)
        initial = lax.slice_in_dim(array, 0, width, axis=dim)
        before = lax.ppermute(last, axis, up)
        after = lax.ppermute(initial, axis, down)
        array = jnp.concatenate([before, array, after], axis=dim)
    return array


def carried_in(part, axis, combine, identity):
    place = lax.axis_index(axis)
    gathered = lax.all_gather(part, axis)
    state = jnp.zeros_like(part) + jnp.asarray(identity, part.dtype)

    def one(hop, state):
        return combine(state, lax.dynamic_index_in_dim(gathered, hop, 0, False))

    return lax.fori_loop(0, place, one, state)


def without_rim(values, dims):
    for dim in dims:
        values = lax.slice_in_dim(values, 1, values.shape[dim] - 1, axis=dim)
    return values


def shifted_cells(values, dim, start, dims):
    others = [other for other in dims if other != dim]
    values = without_rim(values, others)
    return lax.slice_in_dim(values, start, start + values.shape[dim] - 2, axis=dim)


def march_step(padded, flow_y, flow_x, flow_z):
    middle = without_rim(padded, (0, 1, 2))
    lower = [shifted_cells(padded, dim, 0, (0, 1, 2)) for dim in (0, 1, 2)]
    upper = [shifted_cells(padded, dim, 2, (0, 1, 2)) for dim in (0, 1, 2)]
    slopes = [above - below for above, below in zip(upper, lower)]
    smooth_rate = 0.05
    spread = lower[0] + upper[0] + lower[1] + upper[1] + lower[2] + upper[2] - 6.0 * middle
    return (
        middle - flow_y * slopes[0] - flow_x * slopes[1] - flow_z * slopes[2] + smooth_rate * spread
    )


def local(field_values, flow_y, flow_x, flow_z):
    for step in range(STEPS):
        padded = extended(field_values, (("south", 0), ("east", 1), ("down", 2)), 1)
        field_values = march_step(padded, flow_y, flow_x, flow_z)
    here = jnp.cumsum(field_values, axis=2)
    total = lax.slice_in_dim(here, here.shape[2] - 1, here.shape[2], axis=2)

    def add_pair(earlier_total, later_total):
        return earlier_total + later_total

    below = carried_in(total, "down", add_pair, jnp.zeros_like(total))
    potential = (here + below) / (field_values.shape[2] * lax.axis_size("down"))
    return (potential, field_values)


def solution(mesh):
    return jax.shard_map(
        local,
        mesh=mesh,
        in_specs=(
            P("south", "east", "down", None),
            P("south", "east", "down", None),
            P("south", "east", "down", None),
            P("south", "east", "down", None),
        ),
        out_specs=(P("south", "east", "down", None), P("south", "east", "down", None)),
        check_vma=False,
    )
```

profile of v0, /device:TPU:1, one launch (start us, length us, event | category | flops | bytes accessed | tf_op | source)
XLA Modules:
  0.0 174.0 jit_solution(9019068158788917898)
XLA Ops:
  0.6 2.6 %copy.12 = f32[8,96,8,128]{3,1,2,0:T(8,128)S(1)} copy(f32[8,96,8,128]{3,2,1,0:T(8,128)} %param.6) | data formatting | bytes 6291456 | tf_op args[0]
  3.3 2.1 %collective-permute-start.1 = (f32[1,96,8,128]{3,1,2,0:T(8,128)S(1)}, f32[1,96,8,128]{3,1,2,0:T(8,128)S(1)}, u32[]{:S(2)}, u32[]{:S(2)}) collective-permute-start(f32[1,96,8,128]{3,1,2,0:T(8,128)S(1)} %get-tuple-element.67), channel_id=1, source_target_pairs={{0,8},{8,16},{16,24},{24,0},{1,9},{9,17},{17,25},{25,1},{2,10},{10... | collective-permute-start | bytes 1179656 | tf_op jit(solution)/shard_map/ppermute | solution.py:16
  5.4 1.0 collective-permute-start
  6.4 8.8 %collective-permute-done.1 = f32[1,96,8,128]{3,1,2,0:T(8,128)S(1)} collective-permute-done((f32[1,96,8,128]{3,1,2,0:T(8,128)S(1)}, f32[1,96,8,128]{3,1,2,0:T(8,128)S(1)}, u32[]{:S(2)}, u32[]{:S(2)}) %collective-permute-start.1) | collective-permute-done | bytes 393248 | tf_op jit(solution)/shard_map/ppermute | solution.py:16
  15.2 0.6 constant_dynamic-update-slice_fusion.1
  15.8 7.7 %collective-permute-done = f32[1,96,8,128]{3,1,2,0:T(8,128)S(1)} collective-permute-done((f32[1,96,8,128]{3,1,2,0:T(8,128)S(1)}, f32[1,96,8,128]{3,1,2,0:T(8,128)S(1)}, u32[]{:S(2)}, u32[]{:S(2)}) %collective-permute-start) | collective-permute-done | bytes 393248 | tf_op jit(solution)/shard_map/ppermute | solution.py:17
  23.7 3.4 %collective-permute-start.2 = (f32[10,1,8,128]{3,1,2,0:T(1,128)S(1)}, f32[10,1,8,128]{3,1,2,0:T(1,128)S(1)}, u32[]{:S(2)}, u32[]{:S(2)}) collective-permute-start(f32[10,1,8,128]{3,1,2,0:T(1,128)S(1)} %get-tuple-element.59), channel_id=1, source_target_pairs={{2,0},{4,2},{6,4},{0,6},{3,1},{5,3},{7,5},{1,7},{10,8},{12,10},{14... | collective-permute-start | bytes 122888 | tf_op jit(solution)/shard_map/ppermute | solution.py:17
  27.0 1.1 collective-permute-done.2
  28.1 3.5 %collective-permute-done.3 = f32[10,1,8,128]{3,1,2,0:T(1,128)S(1)} collective-permute-done((f32[10,1,8,128]{3,1,2,0:T(1,128)S(1)}, f32[10,1,8,128]{3,1,2,0:T(1,128)S(1)}, u32[]{:S(2)}, u32[]{:S(2)}) %collective-permute-start.3) | collective-permute-done | bytes 40992 | tf_op jit(solution)/shard_map/ppermute | solution.py:16
  31.7 0.1 pad_maximum_fusion.79
  31.8 3.0 %collective-permute-start.4 = (f32[10,98,1,128]{3,1,2,0:T(8,128)S(1)}, f32[10,98,1,128]{3,1,2,0:T(8,128)S(1)}, u32[]{:S(2)}, u32[]{:S(2)}) collective-permute-start(f32[10,98,1,128]{3,1,2,0:T(8,128)S(1)} %get-tuple-element.51), channel_id=1, source_target_pairs={{1,0},{0,1},{3,2},{2,3},{5,4},{4,5},{7,6},{6,7},{9,8},{8,9},{11,10... | collective-permute-start | bytes 1505288 | tf_op jit(solution)/shard_map/ppermute | solution.py:17
  34.8 0.1 collective-permute-start.5
  34.9 1.5 collective-permute-done.4
  36.4 0.8 collective-permute-done.5
  37.1 9.8 %multiply_add_fusion.3 = f32[8,96,8,128]{3,1,2,0:T(8,128)S(1)} fusion(f32[8,96,8,128]{3,1,2,0:T(8,128)} %copy-done.3, f32[10,98,1,128]{3,1,2,0:T(8,128)S(1)} %collective-permute-done.4, f32[10,1,8,128]{3,1,2,0:T(1,128)S(1)} %collective-permute-done.2, f32[10,96,8,128]{3,1,2,0:T(8,128)S(1)} %constant_dynamic-update-slice_fusion, ...), kind=kLoop, calls=%fused_computation.69 | loop fusion | flops 22020096 | bytes 21532672 | tf_op jit(solution)/shard_map/add | solution.py:53
  47.0 1.2 collective-permute-start.6
  48.2 0.3 collective-permute-start.7
  48.5 8.8 %collective-permute-done.6 = f32[1,96,8,128]{3,1,2,0:T(8,128)S(1)} collective-permute-done((f32[1,96,8,128]{3,1,2,0:T(8,128)S(1)}, f32[1,96,8,128]{3,1,2,0:T(8,128)S(1)}, u32[]{:S(2)}, u32[]{:S(2)}) %collective-permute-start.6) | collective-permute-done | bytes 393248 | tf_op jit(solution)/shard_map/ppermute | solution.py:17
  57.3 8.4 %collective-permute-done.7 = f32[1,96,8,128]{3,1,2,0:T(8,128)S(1)} collective-permute-done((f32[1,96,8,128]{3,1,2,0:T(8,128)S(1)}, f32[1,96,8,128]{3,1,2,0:T(8,128)S(1)}, u32[]{:S(2)}, u32[]{:S(2)}) %collective-permute-start.7) | collective-permute-done | bytes 393248 | tf_op jit(solution)/shard_map/ppermute | solution.py:16
  65.7 0.1 pad_maximum_fusion.88
  65.8 1.5 collective-permute-start.9
  67.3 1.4 collective-permute-done.8
  68.7 2.0 %collective-permute-done.9 = f32[10,1,8,128]{3,1,2,0:T(1,128)S(1)} collective-permute-done((f32[10,1,8,128]{3,1,2,0:T(1,128)S(1)}, f32[10,1,8,128]{3,1,2,0:T(1,128)S(1)}, u32[]{:S(2)}, u32[]{:S(2)}) %collective-permute-start.9) | collective-permute-done | bytes 40992 | tf_op jit(solution)/shard_map/ppermute | solution.py:16
  70.6 0.1 pad_maximum_fusion.74
  70.7 2.4 %collective-permute-start.10 = (f32[10,98,1,128]{3,1,2,0:T(8,128)S(1)}, f32[10,98,1,128]{3,1,2,0:T(8,128)S(1)}, u32[]{:S(2)}, u32[]{:S(2)}) collective-permute-start(f32[10,98,1,128]{3,1,2,0:T(8,128)S(1)} %get-tuple-element.49), channel_id=1, source_target_pairs={{1,0},{0,1},{3,2},{2,3},{5,4},{4,5},{7,6},{6,7},{9,8},{8,9},{11,10... | collective-permute-start | bytes 1505288 | tf_op jit(solution)/shard_map/ppermute | solution.py:17
  73.1 0.1 collective-permute-start.11
  73.2 1.5 collective-permute-done.10
  74.7 0.8 collective-permute-done.11
  75.4 7.7 %multiply_add_fusion.2 = f32[8,96,8,128]{3,1,2,0:T(8,128)S(1)} fusion(f32[8,96,8,128]{3,1,2,0:T(8,128)S(1)} %multiply_add_fusion.3, f32[10,98,1,128]{3,1,2,0:T(8,128)S(1)} %collective-permute-done.10, f32[10,1,8,128]{3,1,2,0:T(1,128)S(1)} %collective-permute-done.8, f32[1,96,8,128]{3,1,2,0:T(8,128)S(1)} %collective-permute-done.6, ...), kind=kLoop, calls=%fused_computation.68 | loop fusion | flops 28311552 | bytes 17600512 | tf_op jit(solution)/shard_map/add | solution.py:53
  83.2 2.2 %collective-permute-start.12 = (f32[1,96,8,128]{3,1,2,0:T(8,128)S(1)}, f32[1,96,8,128]{3,1,2,0:T(8,128)S(1)}, u32[]{:S(2)}, u32[]{:S(2)}) collective-permute-start(f32[1,96,8,128]{3,1,2,0:T(8,128)S(1)} %get-tuple-element.63), channel_id=1, source_target_pairs={{8,0},{16,8},{24,16},{0,24},{9,1},{17,9},{25,17},{1,25},{10,2},{18... | collective-permute-start | bytes 1179656 | tf_op jit(solution)/shard_map/ppermute | solution.py:17
  85.4 8.1 %collective-permute-done.12 = f32[1,96,8,128]{3,1,2,0:T(8,128)S(1)} collective-permute-done((f32[1,96,8,128]{3,1,2,0:T(8,128)S(1)}, f32[1,96,8,128]{3,1,2,0:T(8,128)S(1)}, u32[]{:S(2)}, u32[]{:S(2)}) %collective-permute-start.12) | collective-permute-done | bytes 393248 | tf_op jit(solution)/shard_map/ppermute | solution.py:17
  93.6 9.4 %collective-permute-done.13 = f32[1,96,8,128]{3,1,2,0:T(8,128)S(1)} collective-permute-done((f32[1,96,8,128]{3,1,2,0:T(8,128)S(1)}, f32[1,96,8,128]{3,1,2,0:T(8,128)S(1)}, u32[]{:S(2)}, u32[]{:S(2)}) %collective-permute-start.13) | collective-permute-done | bytes 393248 | tf_op jit(solution)/shard_map/ppermute | solution.py:16
  103.0 0.1 collective-permute-start.14
  103.1 1.4 collective-permute-start.15
  104.5 1.4 collective-permute-done.14
  105.9 2.0 %collective-permute-done.15 = f32[10,1,8,128]{3,1,2,0:T(1,128)S(1)} collective-permute-done((f32[10,1,8,128]{3,1,2,0:T(1,128)S(1)}, f32[10,1,8,128]{3,1,2,0:T(1,128)S(1)}, u32[]{:S(2)}, u32[]{:S(2)}) %collective-permute-start.15) | collective-permute-done | bytes 40992 | tf_op jit(solution)/shard_map/ppermute | solution.py:16
  107.9 0.1 pad_maximum_fusion.69
  108.0 2.6 %collective-permute-start.16 = (f32[10,98,1,128]{3,1,2,0:T(8,128)S(1)}, f32[10,98,1,128]{3,1,2,0:T(8,128)S(1)}, u32[]{:S(2)}, u32[]{:S(2)}) collective-permute-start(f32[10,98,1,128]{3,1,2,0:T(8,128)S(1)} %get-tuple-element.47), channel_id=1, source_target_pairs={{1,0},{0,1},{3,2},{2,3},{5,4},{4,5},{7,6},{6,7},{9,8},{8,9},{11,10... | collective-permute-start | bytes 1505288 | tf_op jit(solution)/shard_map/ppermute | solution.py:17
  110.6 0.1 collective-permute-start.17
  110.7 1.5 collective-permute-done.16
  112.2 0.8 collective-permute-done.17
  112.9 7.8 %multiply_add_fusion.1 = f32[8,96,8,128]{3,1,2,0:T(8,128)S(1)} fusion(f32[8,96,8,128]{3,1,2,0:T(8,128)S(1)} %multiply_add_fusion.2, f32[10,98,1,128]{3,1,2,0:T(8,128)S(1)} %collective-permute-done.16, f32[10,1,8,128]{3,1,2,0:T(1,128)S(1)} %collective-permute-done.14, f32[1,96,8,128]{3,1,2,0:T(8,128)S(1)} %collective-permute-done.12, ...), kind=kLoop, calls=%fused_computation.67 | loop fusion | flops 28311552 | bytes 17600512 | tf_op jit(solution)/shard_map/add | solution.py:53
  120.8 1.2 collective-permute-start.18
  122.0 0.3 collective-permute-start.19
  122.3 8.8 %collective-permute-done.18 = f32[1,96,8,128]{3,1,2,0:T(8,128)S(1)} collective-permute-done((f32[1,96,8,128]{3,1,2,0:T(8,128)S(1)}, f32[1,96,8,128]{3,1,2,0:T(8,128)S(1)}, u32[]{:S(2)}, u32[]{:S(2)}) %collective-permute-start.18) | collective-permute-done | bytes 393248 | tf_op jit(solution)/shard_map/ppermute | solution.py:17
  131.1 8.4 %collective-permute-done.19 = f32[1,96,8,128]{3,1,2,0:T(8,128)S(1)} collective-permute-done((f32[1,96,8,128]{3,1,2,0:T(8,128)S(1)}, f32[1,96,8,128]{3,1,2,0:T(8,128)S(1)}, u32[]{:S(2)}, u32[]{:S(2)}) %collective-permute-start.19) | collective-permute-done | bytes 393248 | tf_op jit(solution)/shard_map/ppermute | solution.py:16
  139.6 1.5 collective-permute-start.21
  141.1 1.4 collective-permute-done.20
  142.5 2.1 %collective-permute-done.21 = f32[10,1,8,128]{3,1,2,0:T(1,128)S(1)} collective-permute-done((f32[10,1,8,128]{3,1,2,0:T(1,128)S(1)}, f32[10,1,8,128]{3,1,2,0:T(1,128)S(1)}, u32[]{:S(2)}, u32[]{:S(2)}) %collective-permute-start.21) | collective-permute-done | bytes 40992 | tf_op jit(solution)/shard_map/ppermute | solution.py:16
  144.6 1.1 pad_maximum_fusion.64
  145.7 2.3 %collective-permute-start.22 = (f32[10,98,1,128]{3,1,2,0:T(8,128)}, f32[10,98,1,128]{3,1,2,0:T(8,128)}, u32[]{:S(2)}, u32[]{:S(2)}) collective-permute-start(f32[10,98,1,128]{3,1,2,0:T(8,128)} %get-tuple-element.45), channel_id=1, source_target_pairs={{1,0},{0,1},{3,2},{2,3},{5,4},{4,5},{7,6},{6,7},{9,8},{8,9},{11,10... | collective-permute-start | bytes 1505288 | tf_op jit(solution)/shard_map/ppermute | solution.py:17
  148.0 0.1 collective-permute-start.23
  148.1 1.8 %collective-permute-done.22 = f32[10,98,1,128]{3,1,2,0:T(8,128)} collective-permute-done((f32[10,98,1,128]{3,1,2,0:T(8,128)}, f32[10,98,1,128]{3,1,2,0:T(8,128)}, u32[]{:S(2)}, u32[]{:S(2)}) %collective-permute-start.22) | collective-permute-done | bytes 501792 | tf_op jit(solution)/shard_map/ppermute | solution.py:17
  149.9 0.8 collective-permute-done.23
  150.6 8.5 %multiply_add_fusion = f32[8,96,8,128]{3,1,2,0:T(8,128)S(1)} fusion(f32[8,96,8,128]{3,1,2,0:T(8,128)S(1)} %multiply_add_fusion.1, f32[10,98,1,128]{3,1,2,0:T(8,128)} %collective-permute-done.22, f32[10,1,8,128]{3,1,2,0:T(1,128)} %copy-done.6, f32[1,96,8,128]{3,1,2,0:T(8,128)S(1)} %collective-permute-done.18, f32[1,96,8,128]{3,1,2,0:T(8,128)} %copy-done.5, ...), kind=kLoop, calls=%fused_computation.66 | loop fusion | flops 28311552 | bytes 17600512 | tf_op jit(solution)/shard_map/add | solution.py:53
  159.2 3.3 %fusion.5 = f32[8,96,8,128]{3,1,2,0:T(8,128)S(1)} fusion(f32[8,96,8,128]{3,1,2,0:T(8,128)S(1)} %multiply_add_fusion), kind=kOutput, calls=%fused_computation.105 | output fusion | flops 5505024 | bytes 6291456 | tf_op jit(solution)/shard_map/jit(cumsum)/reduce_window_sum | solution.py:61
  162.5 3.4 %copy.28 = f32[8,96,8,128]{3,2,1,0:T(8,128)} copy(f32[8,96,8,128]{3,1,2,0:T(8,128)S(1)} %multiply_add_fusion) | data formatting | bytes 6291456
  165.9 2.5 %all-gather = f32[16,96,1,128]{3,1,2,0:T(8,128)} all-gather(f32[8,96,1,128]{3,1,2,0:T(8,128)S(1)} %slice.362), channel_id=2, replica_groups=mesh['south'=4,'east'=4,'down'=2] {'down'}, dimensions={0}, use_global_device_ids=true | all-gather | bytes 1179648 | tf_op jit(solution)/shard_map/all_gather | solution.py:24
  168.4 0.2 broadcast_in_dim.3
  168.7 1.5 while.10
  168.7 1.0 constant_dynamic-slice_fusion.2
  169.7 0.4 add.150
  170.2 0.4 add_multiply_fusion
  170.6 3.4 %copy.27 = f32[8,96,8,128]{3,2,1,0:T(8,128)} copy(f32[8,96,8,128]{3,1,2,0:T(8,128)S(1)} %add_multiply_fusion) | data formatting | bytes 6291456
  (30 shorter events, 0.6 us)
Async XLA Ops:
  0.6 14.6 %copy-start.4 = (f32[8,96,8,128]{3,2,1,0:T(8,128)S(1)}, f32[8,96,8,128]{3,2,1,0:T(8,128)}, u32[]{:S(2)}) copy-start(f32[8,96,8,128]{3,2,1,0:T(8,128)} %param.6) | copy-start | bytes 9437188
  3.2 12.6 %copy-start.3 = (f32[8,96,8,128]{3,1,2,0:T(8,128)}, f32[8,96,8,128]{3,1,2,0:T(8,128)S(1)}, u32[]{:S(2)}) copy-start(f32[8,96,8,128]{3,1,2,0:T(8,128)S(1)} %copy.12) | copy-start | bytes 9437188
  3.3 11.9 %collective-permute-start.1 = (f32[1,96,8,128]{3,1,2,0:T(8,128)S(1)}, f32[1,96,8,128]{3,1,2,0:T(8,128)S(1)}, u32[]{:S(2)}, u32[]{:S(2)}) collective-permute-start(f32[1,96,8,128]{3,1,2,0:T(8,128)S(1)} %get-tuple-element.67), channel_id=1, source_target_pairs={{0,8},{8,16},{16,24},{24,0},{1,9},{9,17},{17,25},{25,1},{2,10},{10... | collective-permute-start | bytes 1179656 | tf_op jit(solution)/shard_map/ppermute | solution.py:16
  5.4 18.2 %collective-permute-start = (f32[1,96,8,128]{3,1,2,0:T(8,128)S(1)}, f32[1,96,8,128]{3,1,2,0:T(8,128)S(1)}, u32[]{:S(2)}, u32[]{:S(2)}) collective-permute-start(f32[1,96,8,128]{3,1,2,0:T(8,128)S(1)} %get-tuple-element.66), channel_id=1, source_target_pairs={{8,0},{16,8},{24,16},{0,24},{9,1},{17,9},{25,17},{1,25},{10,2},{18... | collective-permute-start | bytes 1179656 | tf_op jit(solution)/shard_map/ppermute | solution.py:17
  15.2 21.9 %copy-start.1 = (f32[8,96,8,128]{3,2,1,0:T(8,128)S(1)}, f32[8,96,8,128]{3,2,1,0:T(8,128)}, u32[]{:S(2)}) copy-start(f32[8,96,8,128]{3,2,1,0:T(8,128)} %param.8) | copy-start | bytes 9437188
  15.2 21.9 %copy-start.2 = (f32[8,96,8,128]{3,2,1,0:T(8,128)S(1)}, f32[8,96,8,128]{3,2,1,0:T(8,128)}, u32[]{:S(2)}) copy-start(f32[8,96,8,128]{3,2,1,0:T(8,128)} %param.7) | copy-start | bytes 9437188
  15.8 21.3 %copy-start = (f32[8,96,8,128]{3,2,1,0:T(8,128)S(1)}, f32[8,96,8,128]{3,2,1,0:T(8,128)}, u32[]{:S(2)}) copy-start(f32[8,96,8,128]{3,2,1,0:T(8,128)} %param.9) | copy-start | bytes 9437188
  23.7 4.5 %collective-permute-start.2 = (f32[10,1,8,128]{3,1,2,0:T(1,128)S(1)}, f32[10,1,8,128]{3,1,2,0:T(1,128)S(1)}, u32[]{:S(2)}, u32[]{:S(2)}) collective-permute-start(f32[10,1,8,128]{3,1,2,0:T(1,128)S(1)} %get-tuple-element.59), channel_id=1, source_target_pairs={{2,0},{4,2},{6,4},{0,6},{3,1},{5,3},{7,5},{1,7},{10,8},{12,10},{14... | collective-permute-start | bytes 122888 | tf_op jit(solution)/shard_map/ppermute | solution.py:17
  27.0 4.7 %collective-permute-start.3 = (f32[10,1,8,128]{3,1,2,0:T(1,128)S(1)}, f32[10,1,8,128]{3,1,2,0:T(1,128)S(1)}, u32[]{:S(2)}, u32[]{:S(2)}) collective-permute-start(f32[10,1,8,128]{3,1,2,0:T(1,128)S(1)} %get-tuple-element.58), channel_id=1, source_target_pairs={{0,2},{2,4},{4,6},{6,0},{1,3},{3,5},{5,7},{7,1},{8,10},{10,12},{12... | collective-permute-start | bytes 122888 | tf_op jit(solution)/shard_map/ppermute | solution.py:16
  31.8 4.6 %collective-permute-start.4 = (f32[10,98,1,128]{3,1,2,0:T(8,128)S(1)}, f32[10,98,1,128]{3,1,2,0:T(8,128)S(1)}, u32[]{:S(2)}, u32[]{:S(2)}) collective-permute-start(f32[10,98,1,128]{3,1,2,0:T(8,128)S(1)} %get-tuple-element.51), channel_id=1, source_target_pairs={{1,0},{0,1},{3,2},{2,3},{5,4},{4,5},{7,6},{6,7},{9,8},{8,9},{11,10... | collective-permute-start | bytes 1505288 | tf_op jit(solution)/shard_map/ppermute | solution.py:17
  34.8 2.3 %collective-permute-start.5 = (f32[10,98,1,128]{3,1,2,0:T(8,128)S(1)}, f32[10,98,1,128]{3,1,2,0:T(8,128)S(1)}, u32[]{:S(2)}, u32[]{:S(2)}) collective-permute-start(f32[10,98,1,128]{3,1,2,0:T(8,128)S(1)} %get-tuple-element.50), channel_id=1, source_target_pairs={{0,1},{1,0},{2,3},{3,2},{4,5},{5,4},{6,7},{7,6},{8,9},{9,8},{10,11... | collective-permute-start | bytes 1505288 | tf_op jit(solution)/shard_map/ppermute | solution.py:16
  47.0 10.3 %collective-permute-start.6 = (f32[1,96,8,128]{3,1,2,0:T(8,128)S(1)}, f32[1,96,8,128]{3,1,2,0:T(8,128)S(1)}, u32[]{:S(2)}, u32[]{:S(2)}) collective-permute-start(f32[1,96,8,128]{3,1,2,0:T(8,128)S(1)} %get-tuple-element.65), channel_id=1, source_target_pairs={{8,0},{16,8},{24,16},{0,24},{9,1},{17,9},{25,17},{1,25},{10,2},{18... | collective-permute-start | bytes 1179656 | tf_op jit(solution)/shard_map/ppermute | solution.py:17
  48.2 17.5 %collective-permute-start.7 = (f32[1,96,8,128]{3,1,2,0:T(8,128)S(1)}, f32[1,96,8,128]{3,1,2,0:T(8,128)S(1)}, u32[]{:S(2)}, u32[]{:S(2)}) collective-permute-start(f32[1,96,8,128]{3,1,2,0:T(8,128)S(1)} %get-tuple-element.64), channel_id=1, source_target_pairs={{0,8},{8,16},{16,24},{24,0},{1,9},{9,17},{17,25},{25,1},{2,10},{10... | collective-permute-start | bytes 1179656 | tf_op jit(solution)/shard_map/ppermute | solution.py:16
  65.8 2.9 %collective-permute-start.8 = (f32[10,1,8,128]{3,1,2,0:T(1,128)S(1)}, f32[10,1,8,128]{3,1,2,0:T(1,128)S(1)}, u32[]{:S(2)}, u32[]{:S(2)}) collective-permute-start(f32[10,1,8,128]{3,1,2,0:T(1,128)S(1)} %get-tuple-element.57), channel_id=1, source_target_pairs={{2,0},{4,2},{6,4},{0,6},{3,1},{5,3},{7,5},{1,7},{10,8},{12,10},{14... | collective-permute-start | bytes 122888 | tf_op jit(solution)/shard_map/ppermute | solution.py:17
  65.8 4.8 %collective-permute-start.9 = (f32[10,1,8,128]{3,1,2,0:T(1,128)S(1)}, f32[10,1,8,128]{3,1,2,0:T(1,128)S(1)}, u32[]{:S(2)}, u32[]{:S(2)}) collective-permute-start(f32[10,1,8,128]{3,1,2,0:T(1,128)S(1)} %get-tuple-element.56), channel_id=1, source_target_pairs={{0,2},{2,4},{4,6},{6,0},{1,3},{3,5},{5,7},{7,1},{8,10},{10,12},{12... | collective-permute-start | bytes 122888 | tf_op jit(solution)/shard_map/ppermute | solution.py:16
  70.7 3.9 %collective-permute-start.10 = (f32[10,98,1,128]{3,1,2,0:T(8,128)S(1)}, f32[10,98,1,128]{3,1,2,0:T(8,128)S(1)}, u32[]{:S(2)}, u32[]{:S(2)}) collective-permute-start(f32[10,98,1,128]{3,1,2,0:T(8,128)S(1)} %get-tuple-element.49), channel_id=1, source_target_pairs={{1,0},{0,1},{3,2},{2,3},{5,4},{4,5},{7,6},{6,7},{9,8},{8,9},{11,10... | collective-permute-start | bytes 1505288 | tf_op jit(solution)/shard_map/ppermute | solution.py:17
  73.1 2.3 %collective-permute-start.11 = (f32[10,98,1,128]{3,1,2,0:T(8,128)S(1)}, f32[10,98,1,128]{3,1,2,0:T(8,128)S(1)}, u32[]{:S(2)}, u32[]{:S(2)}) collective-permute-start(f32[10,98,1,128]{3,1,2,0:T(8,128)S(1)} %get-tuple-element.48), channel_id=1, source_target_pairs={{0,1},{1,0},{2,3},{3,2},{4,5},{5,4},{6,7},{7,6},{8,9},{9,8},{10,11... | collective-permute-start | bytes 1505288 | tf_op jit(solution)/shard_map/ppermute | solution.py:16
  83.2 10.4 %collective-permute-start.12 = (f32[1,96,8,128]{3,1,2,0:T(8,128)S(1)}, f32[1,96,8,128]{3,1,2,0:T(8,128)S(1)}, u32[]{:S(2)}, u32[]{:S(2)}) collective-permute-start(f32[1,96,8,128]{3,1,2,0:T(8,128)S(1)} %get-tuple-element.63), channel_id=1, source_target_pairs={{8,0},{16,8},{24,16},{0,24},{9,1},{17,9},{25,17},{1,25},{10,2},{18... | collective-permute-start | bytes 1179656 | tf_op jit(solution)/shard_map/ppermute | solution.py:17
  85.4 17.5 %collective-permute-start.13 = (f32[1,96,8,128]{3,1,2,0:T(8,128)S(1)}, f32[1,96,8,128]{3,1,2,0:T(8,128)S(1)}, u32[]{:S(2)}, u32[]{:S(2)}) collective-permute-start(f32[1,96,8,128]{3,1,2,0:T(8,128)S(1)} %get-tuple-element.62), channel_id=1, source_target_pairs={{0,8},{8,16},{16,24},{24,0},{1,9},{9,17},{17,25},{25,1},{2,10},{10... | collective-permute-start | bytes 1179656 | tf_op jit(solution)/shard_map/ppermute | solution.py:16
  103.0 2.9 %collective-permute-start.14 = (f32[10,1,8,128]{3,1,2,0:T(1,128)S(1)}, f32[10,1,8,128]{3,1,2,0:T(1,128)S(1)}, u32[]{:S(2)}, u32[]{:S(2)}) collective-permute-start(f32[10,1,8,128]{3,1,2,0:T(1,128)S(1)} %get-tuple-element.55), channel_id=1, source_target_pairs={{2,0},{4,2},{6,4},{0,6},{3,1},{5,3},{7,5},{1,7},{10,8},{12,10},{14... | collective-permute-start | bytes 122888 | tf_op jit(solution)/shard_map/ppermute | solution.py:17
  103.1 4.8 %collective-permute-start.15 = (f32[10,1,8,128]{3,1,2,0:T(1,128)S(1)}, f32[10,1,8,128]{3,1,2,0:T(1,128)S(1)}, u32[]{:S(2)}, u32[]{:S(2)}) collective-permute-start(f32[10,1,8,128]{3,1,2,0:T(1,128)S(1)} %get-tuple-element.54), channel_id=1, source_target_pairs={{0,2},{2,4},{4,6},{6,0},{1,3},{3,5},{5,7},{7,1},{8,10},{10,12},{12... | collective-permute-start | bytes 122888 | tf_op jit(solution)/shard_map/ppermute | solution.py:16
  108.0 4.2 %collective-permute-start.16 = (f32[10,98,1,128]{3,1,2,0:T(8,128)S(1)}, f32[10,98,1,128]{3,1,2,0:T(8,128)S(1)}, u32[]{:S(2)}, u32[]{:S(2)}) collective-permute-start(f32[10,98,1,128]{3,1,2,0:T(8,128)S(1)} %get-tuple-element.47), channel_id=1, source_target_pairs={{1,0},{0,1},{3,2},{2,3},{5,4},{4,5},{7,6},{6,7},{9,8},{8,9},{11,10... | collective-permute-start | bytes 1505288 | tf_op jit(solution)/shard_map/ppermute | solution.py:17
  110.6 2.3 %collective-permute-start.17 = (f32[10,98,1,128]{3,1,2,0:T(8,128)S(1)}, f32[10,98,1,128]{3,1,2,0:T(8,128)S(1)}, u32[]{:S(2)}, u32[]{:S(2)}) collective-permute-start(f32[10,98,1,128]{3,1,2,0:T(8,128)S(1)} %get-tuple-element.46), channel_id=1, source_target_pairs={{0,1},{1,0},{2,3},{3,2},{4,5},{5,4},{6,7},{7,6},{8,9},{9,8},{10,11... | collective-permute-start | bytes 1505288 | tf_op jit(solution)/shard_map/ppermute | solution.py:16
  120.8 10.4 %collective-permute-start.18 = (f32[1,96,8,128]{3,1,2,0:T(8,128)S(1)}, f32[1,96,8,128]{3,1,2,0:T(8,128)S(1)}, u32[]{:S(2)}, u32[]{:S(2)}) collective-permute-start(f32[1,96,8,128]{3,1,2,0:T(8,128)S(1)} %get-tuple-element.61), channel_id=1, source_target_pairs={{8,0},{16,8},{24,16},{0,24},{9,1},{17,9},{25,17},{1,25},{10,2},{18... | collective-permute-start | bytes 1179656 | tf_op jit(solution)/shard_map/ppermute | solution.py:17
  122.0 17.5 %collective-permute-start.19 = (f32[1,96,8,128]{3,1,2,0:T(8,128)S(1)}, f32[1,96,8,128]{3,1,2,0:T(8,128)S(1)}, u32[]{:S(2)}, u32[]{:S(2)}) collective-permute-start(f32[1,96,8,128]{3,1,2,0:T(8,128)S(1)} %get-tuple-element.60), channel_id=1, source_target_pairs={{0,8},{8,16},{16,24},{24,0},{1,9},{9,17},{17,25},{25,1},{2,10},{10... | collective-permute-start | bytes 1179656 | tf_op jit(solution)/shard_map/ppermute | solution.py:16
  139.5 6.2 %copy-start.5 = (f32[1,96,8,128]{3,1,2,0:T(8,128)}, f32[1,96,8,128]{3,1,2,0:T(8,128)S(1)}, u32[]{:S(2)}) copy-start(f32[1,96,8,128]{3,1,2,0:T(8,128)S(1)} %collective-permute-done.19) | copy-start | bytes 1179652
  139.6 2.9 %collective-permute-start.20 = (f32[10,1,8,128]{3,1,2,0:T(1,128)S(1)}, f32[10,1,8,128]{3,1,2,0:T(1,128)S(1)}, u32[]{:S(2)}, u32[]{:S(2)}) collective-permute-start(f32[10,1,8,128]{3,1,2,0:T(1,128)S(1)} %get-tuple-element.53), channel_id=1, source_target_pairs={{2,0},{4,2},{6,4},{0,6},{3,1},{5,3},{7,5},{1,7},{10,8},{12,10},{14... | collective-permute-start | bytes 122888 | tf_op jit(solution)/shard_map/ppermute | solution.py:17
  139.6 5.0 %collective-permute-start.21 = (f32[10,1,8,128]{3,1,2,0:T(1,128)S(1)}, f32[10,1,8,128]{3,1,2,0:T(1,128)S(1)}, u32[]{:S(2)}, u32[]{:S(2)}) collective-permute-start(f32[10,1,8,128]{3,1,2,0:T(1,128)S(1)} %get-tuple-element.52), channel_id=1, source_target_pairs={{0,2},{2,4},{4,6},{6,0},{1,3},{3,5},{5,7},{7,1},{8,10},{10,12},{12... | collective-permute-start | bytes 122888 | tf_op jit(solution)/shard_map/ppermute | solution.py:16
  142.5 3.2 %copy-start.6 = (f32[10,1,8,128]{3,1,2,0:T(1,128)}, f32[10,1,8,128]{3,1,2,0:T(1,128)S(1)}, u32[]{:S(2)}) copy-start(f32[10,1,8,128]{3,1,2,0:T(1,128)S(1)} %collective-permute-done.20) | copy-start | bytes 122884
  144.6 3.4 %copy-start.7 = (f32[10,1,8,128]{3,1,2,0:T(1,128)}, f32[10,1,8,128]{3,1,2,0:T(1,128)S(1)}, u32[]{:S(2)}) copy-start(f32[10,1,8,128]{3,1,2,0:T(1,128)S(1)} %collective-permute-done.21) | copy-start | bytes 122884
  145.7 4.2 %collective-permute-start.22 = (f32[10,98,1,128]{3,1,2,0:T(8,128)}, f32[10,98,1,128]{3,1,2,0:T(8,128)}, u32[]{:S(2)}, u32[]{:S(2)}) collective-permute-start(f32[10,98,1,128]{3,1,2,0:T(8,128)} %get-tuple-element.45), channel_id=1, source_target_pairs={{1,0},{0,1},{3,2},{2,3},{5,4},{4,5},{7,6},{6,7},{9,8},{8,9},{11,10... | collective-permute-start | bytes 1505288 | tf_op jit(solution)/shard_map/ppermute | solution.py:17
  148.0 2.6 %collective-permute-start.23 = (f32[10,98,1,128]{3,1,2,0:T(8,128)}, f32[10,98,1,128]{3,1,2,0:T(8,128)}, u32[]{:S(2)}, u32[]{:S(2)}) collective-permute-start(f32[10,98,1,128]{3,1,2,0:T(8,128)} %get-tuple-element.44), channel_id=1, source_target_pairs={{0,1},{1,0},{2,3},{3,2},{4,5},{5,4},{6,7},{7,6},{8,9},{9,8},{10,11... | collective-permute-start | bytes 1505288 | tf_op jit(solution)/shard_map/ppermute | solution.py:16
where the time goes:
time: 174 us
  waiting for transfers between devices  92.5 us (53%)
  other arithmetic  39.5 us (23%)
  starting transfers between devices  26.9 us (15%)
  local copies, waits for them, and re-layouts  11.7 us (7%)
  blocking collectives  2.5 us (1%)
    ppermute x12, waiting for transfers between devices, extended(): before = lax.ppermute(last, axis, up)  47.5 us
    ppermute x12, waiting for transfers between devices, extended(): after = lax.ppermute(initial, axis, down)  45 us
    add x4, other arithmetic, march_step(): middle - flow_y * slopes[0] - flow_x * slopes[1] - flow_z * slopes[2]  33.9 us
    ppermute x12, starting transfers between devices, extended(): after = lax.ppermute(initial, axis, down)  19.6 us
    unnamed x21, local copies, waits for them, and re-layouts  10.1 us
    ppermute x12, starting transfers between devices, extended(): before = lax.ppermute(last, axis, up)  7.32 us
  transfers between devices with their start and end apart: 24, of which 24 were waited for; matrix products, arithmetic and copies ran while one was open for 0% of the time, Pallas kernels for 0%

commit v1 on v0

v1 whole, which is shorter than its diff:
```python
import functools

import jax
import jax.numpy as jnp
from jax import lax
from jax.experimental import pallas as pl
from jax.experimental.pallas import tpu as pltpu
from jax.sharding import PartitionSpec as P

STEPS = 4
AXES = ("south", "east", "down")
MESH = pl.DeviceIdType.MESH


def group_of(columns):
    return next(size for size in (8, 4, 2, 1) if columns % size == 0)


def chunk_of(columns, group):
    return next(size for size in (2 * group, group) if columns % size == 0)


def kernel(sizes, depth, field, flow_y, flow_x, flow_z, pot_out, end_out, u, end, pot, fy, fx, fz,
           faces, halos, totals, totals_in, load_sem, store_sem, south_send, south_recv,
           east_send, east_recv, down_send, down_recv, tot_send, tot_recv):
    rows, cells, levels = field.shape
    columns = cells // depth
    group = group_of(columns)
    width = chunk_of(columns, group)
    chunks = columns // width
    places = {axis: lax.axis_index(axis) for axis in AXES}

    def beside(axis, hop):
        return {axis: lax.rem(places[axis] + hop, sizes[axis])}

    hops = [(axis, hop) for axis in ("south", "east") for hop in sorted({1, sizes[axis] - 1})]
    hops += [("down", hop) for hop in range(1, sizes["down"])]
    barrier = pltpu.get_barrier_semaphore()
    for axis, hop in hops:
        pl.semaphore_signal(barrier, inc=1, device_id=beside(axis, hop), device_id_type=MESH)

    flows = ((flow_y, fy), (flow_x, fx), (flow_z, fz))
    loads = [pltpu.make_async_copy(field, u.at[0, pl.ds(1, rows), pl.ds(depth, cells), :], load_sem.at[0])]
    loads += [pltpu.make_async_copy(src, dst, load_sem.at[1 + i]) for i, (src, dst) in enumerate(flows)]
    for load in loads:
        load.start()
    pl.semaphore_wait(barrier, len(hops))

    def south(t, side, c):
        row = rows - 1 if side == 0 else 0
        at = pl.multiple_of(c * width * depth, 8)
        if t == 0:
            src = field.at[row, pl.ds(at, width * depth), :]
        else:
            src = u.at[t, row + 1, pl.ds(at + depth, width * depth), :]
        return pltpu.make_async_remote_copy(
            src_ref=src,
            dst_ref=u.at[t, 0 if side == 0 else rows + 1, pl.ds(at + depth, width * depth), :],
            send_sem=south_send.at[t, side, c], recv_sem=south_recv.at[t, side, c],
            device_id=beside("south", 1 if side == 0 else sizes["south"] - 1), device_id_type=MESH)

    blocks = ((1, rows - 2), (0, 1), (rows - 1, 1))

    def east(t, side, part):
        start, count = blocks[part]
        column = columns if side == 0 else 1
        if t == 0:
            src = field.at[pl.ds(start, count), pl.ds((column - 1) * depth, depth), :]
        else:
            src = u.at[t, pl.ds(start + 1, count), pl.ds(column * depth, depth), :]
        return pltpu.make_async_remote_copy(
            src_ref=src,
            dst_ref=u.at[t, pl.ds(start + 1, count), pl.ds(0 if side == 0 else cells + depth, depth), :],
            send_sem=east_send.at[t, side, part], recv_sem=east_recv.at[t, side, part],
            device_id=beside("east", 1 if side == 0 else sizes["east"] - 1), device_id_type=MESH)

    def down(t, side, part):
        start, count = blocks[part]
        return pltpu.make_async_remote_copy(
            src_ref=faces.at[t, side, pl.ds(start, count)],
            dst_ref=halos.at[t, side, pl.ds(start, count)],
            send_sem=down_send.at[t, side, part], recv_sem=down_recv.at[t, side, part],
            device_id=beside("down", 1 if side == 0 else sizes["down"] - 1), device_id_type=MESH)

    def total(hop, part):
        start, count = blocks[part]
        return pltpu.make_async_remote_copy(
            src_ref=totals.at[pl.ds(start, count)],
            dst_ref=totals_in.at[hop - 1, pl.ds(start, count)],
            send_sem=tot_send.at[hop - 1, part], recv_sem=tot_recv.at[hop - 1, part],
            device_id=beside("down", hop), device_id_type=MESH)

    place_in_block = lax.broadcasted_iota(jnp.int32, (depth, levels), 0)
    on_first, on_last = place_in_block == 0, place_in_block == depth - 1

    def take_faces(t, y, x0):
        for side, place in ((0, depth - 1), (1, 0)):
            start = (x0 + 1) * depth + place
            faces[t, side, y, pl.ds(x0, group), :] = u[t, y + 1, pl.ds(start, group, stride=depth), :]

    def march(t, y, x0):
        def at(x, pad):
            return pl.ds(pl.multiple_of((x + pad) * depth, 8), depth)

        line = [u[t - 1, y + 1, at(x0 + g, 0), :] for g in range(group + 2)]
        for g in range(group):
            x = x0 + g
            mid, west, east_of = line[g + 1], line[g], line[g + 2]
            north, south_of = u[t - 1, y, at(x, 1), :], u[t - 1, y + 2, at(x, 1), :]
            low = jnp.broadcast_to(halos[t - 1, 0, y, pl.ds(x, 1), :], (depth, levels))
            high = jnp.broadcast_to(halos[t - 1, 1, y, pl.ds(x, 1), :], (depth, levels))
            low = jnp.where(on_first, low, pltpu.roll(mid, 1, 0))
            high = jnp.where(on_last, high, pltpu.roll(mid, depth - 1, 0))
            own = at(x, 0)
            spread = (north + south_of) + (west + east_of) + (low + high) - 6.0 * mid
            value = (mid - fy[y, own, :] * (south_of - north) - fx[y, own, :] * (east_of - west)
                     - fz[y, own, :] * (high - low) + 0.05 * spread)
            if t < STEPS:
                u[t, y + 1, at(x, 1), :] = value
            else:
                end[y, own, :] = value
                hop = 1
                while hop < depth:
                    value = value + jnp.where(place_in_block >= hop, pltpu.roll(value, hop, 0), 0.0)
                    hop *= 2
                pot[y, own, :] = value
        if t < STEPS:
            take_faces(t, y, x0)
        else:
            start = x0 * depth + depth - 1
            totals[y, pl.ds(x0, group), :] = pot[y, pl.ds(start, group, stride=depth), :]

    def over(y0, count, x0, span, body):
        groups = span // group

        def one(i, carry):
            body(y0 + i // groups, pl.multiple_of(x0 + (i % groups) * group, group))
            return carry

        lax.fori_loop(0, count * groups, one, 0)

    def finish(part):
        for hop in range(1, sizes["down"]):
            total(hop, part).wait_recv()

        def one(y, x0):
            for g in range(group):
                own = pl.ds(pl.multiple_of((x0 + g) * depth, 8), depth)
                value = pot[y, own, :]
                for hop in range(1, sizes["down"]):
                    below = jnp.broadcast_to(totals_in[hop - 1, y, pl.ds(x0 + g, 1), :], (depth, levels))
                    value = value + jnp.where(places["down"] >= hop, below, 0.0)
                pot[y, own, :] = value / (depth * sizes["down"])

        over(*blocks[part], 0, columns, one)

    def stores(part):
        start, count = blocks[part]
        cut = pl.ds(start, count)
        return (pltpu.make_async_copy(end.at[cut], end_out.at[cut], store_sem.at[0, part]),
                pltpu.make_async_copy(pot.at[cut], pot_out.at[cut], store_sem.at[1, part]))

    def each_chunk(body):
        def one(c, carry):
            body(c)
            return carry

        lax.fori_loop(0, chunks, one, 0)

    def send_chunk(t, c):
        for side in (0, 1):
            south(t, side, c).start()

    each_chunk(lambda c: send_chunk(0, c))
    for part in (0, 1, 2):
        for side in (0, 1):
            east(0, side, part).start()
    loads[0].wait()
    for part in (0, 1, 2):
        over(*blocks[part], 0, columns, functools.partial(take_faces, 0))
        for side in (0, 1):
            down(0, side, part).start()
    for load in loads[1:]:
        load.wait()

    for t in range(1, STEPS + 1):
        for side in (0, 1):
            east(t - 1, side, 0).wait_recv()
            down(t - 1, side, 0).wait_recv()
        over(*blocks[0], 0, columns, functools.partial(march, t))
        if t < STEPS:
            for side in (0, 1):
                east(t, side, 0).start()
                down(t, side, 0).start()
        else:
            stores(0)[0].start()
            for hop in range(1, sizes["down"]):
                total(hop, 0).start()
            finish(0)
            stores(0)[1].start()
        for part in (1, 2):
            for side in (0, 1):
                east(t - 1, side, part).wait_recv()
                down(t - 1, side, part).wait_recv()

        def rim(c):
            for side in (0, 1):
                south(t - 1, side, c).wait_recv()
                y = 0 if side == 0 else rows - 1
                over(y, 1, c * width, width, functools.partial(march, t))
            if t < STEPS:
                send_chunk(t, c)

        each_chunk(rim)
        for part in (1, 2):
            if t < STEPS:
                for side in (0, 1):
                    east(t, side, part).start()
                    down(t, side, part).start()
            else:
                stores(part)[0].start()
                for hop in range(1, sizes["down"]):
                    total(hop, part).start()
    for part in (1, 2):
        finish(part)
        stores(part)[1].start()
    for t in range(STEPS):
        each_chunk(lambda c: [south(t, side, c).wait_send() for side in (0, 1)])
        for part in (0, 1, 2):
            for side in (0, 1):
                east(t, side, part).wait_send()
                down(t, side, part).wait_send()
    for part in (0, 1, 2):
        for hop in range(1, sizes["down"]):
            total(hop, part).wait_send()
        for store in stores(part):
            store.wait()


def local(sizes, field_values, *flows):
    rows, columns, depth, levels = field_values.shape
    cells = columns * depth
    width = chunk_of(columns, group_of(columns))
    flat = [array.reshape(rows, cells, levels) for array in (field_values, *flows)]
    block = pltpu.VMEM((rows, cells, levels), jnp.float32)
    dma = pltpu.SemaphoreType.DMA
    south_sems, side_sems = (STEPS, 2, columns // width), (STEPS, 2, 3)
    others = sizes["down"] - 1
    face = (rows, columns, levels)
    out = jax.ShapeDtypeStruct((rows, cells, levels), jnp.float32)
    results = pl.pallas_call(
        functools.partial(kernel, sizes, depth),
        out_shape=(out, out),
        in_specs=[pl.BlockSpec(memory_space=pl.ANY)] * 4,
        out_specs=(pl.BlockSpec(memory_space=pl.ANY),) * 2,
        scratch_shapes=[
            pltpu.VMEM((STEPS, rows + 2, cells + 2 * depth, levels), jnp.float32),
            block, block, block, block, block,
            pltpu.VMEM((STEPS, 2, *face), jnp.float32),
            pltpu.VMEM((STEPS, 2, *face), jnp.float32),
            pltpu.VMEM(face, jnp.float32),
            pltpu.VMEM((others, *face), jnp.float32),
            dma((4,)), dma((2, 3)),
            dma(south_sems), dma(south_sems),
            dma(side_sems), dma(side_sems),
            dma(side_sems), dma(side_sems),
            dma((others, 3)), dma((others, 3)),
        ],
        compiler_params=pltpu.CompilerParams(
            collective_id=0, has_side_effects=True, vmem_limit_bytes=60 * 1024 * 1024),
    )(*flat)
    return tuple(array.reshape(rows, columns, depth, levels) for array in results)


def solution(mesh):
    spec = P("south", "east", "down", None)
    sizes = {axis: mesh.shape[axis] for axis in AXES}
    return jax.shard_map(
        functools.partial(local, sizes), mesh=mesh, in_specs=(spec,) * 4,
        out_specs=(spec, spec), check_vma=False)
```

time: 174 us -> 85.3 us (0.49)
  waiting for transfers between devices: 92.5 us -> 0 us
  Pallas kernels: 0 us -> 78.9 us
  other arithmetic: 39.5 us -> 0 us
  starting transfers between devices: 26.9 us -> 0 us
  local copies, waits for them, and re-layouts: 11.7 us -> 5.6 us
  blocking collectives: 2.5 us -> 0 us
    ppermute x24 -> x0, waiting for transfers between devices: 92.5 us -> none  [the longest x12 47.5 us: extended(): before = lax.ppermute(last, axis, up)]
    pallas_call x0 -> x1, Pallas kernels: none -> 78.9 us  [local(): pl.pallas_call(functools.partial(kernel, sizes, depth), out_shape=(out, o...]
    add x5 -> x0, other arithmetic: 34.3 us -> none  [the longest x4 33.9 us: march_step(): middle - flow_y * slopes[0] - flow_x * slopes[1] - flow_z * slopes[2]]
    ppermute x24 -> x0, starting transfers between devices: 26.9 us -> none  [the longest x12 19.6 us: extended(): after = lax.ppermute(initial, axis, down)]
    unnamed x21 -> x4, local copies, waits for them, and re-layouts: 10.1 us -> 5.6 us
    another operation x1 -> x0, other arithmetic: 3.29 us -> none  [local(): here = jnp.cumsum(field_values, axis=2)]
    all_gather x1 -> x0, blocking collectives: 2.5 us -> none  [carried_in(): gathered = lax.all_gather(part, axis)]
  transfers between devices with their start and end apart: 24 -> 0, of which waited for: 24 -> 0; matrix products, arithmetic and copies ran while one was open for 0% -> 0% of each run, Pallas kernels for 0% -> 0%
where the time goes in v1:
time: 85.3 us; the launch traced here: 85.2 us
  Pallas kernels  78.9 us (92%)
  local copies, waits for them, and re-layouts  5.6 us (7%)
    pallas_call x1, Pallas kernels, local(): pl.pallas_call(functools.partial(kernel, sizes, depth), out_shape=(out, o...  78.9 us
    unnamed x4, local copies, waits for them, and re-layouts  5.6 us

profile of v1, /device:TPU:1, one launch (start us, length us, event | category | flops | bytes accessed | tf_op | source)
XLA Modules:
  0.0 85.2 jit_solution(7783207346222578240)
XLA Ops:
  0.6 78.9 %shard_map.59 = (f32[8,768,128]{2,1,0:T(8,128)}, f32[8,768,128]{2,1,0:T(8,128)}) custom-call(f32[8,768,128]{2,1,0:T(8,128)} %bitcast.8, f32[8,768,128]{2,1,0:T(8,128)} %bitcast.9, f32[8,768,128]{2,1,0:T(8,128)} %bitcast.10, f32[8,768,128]{2,1,0:T(8,128)} %bitcast.11), custom_call_target="tpu_custom_call" | custom-call | tf_op jit(solution)/shard_map/pallas_call | solution.py:251
  79.5 0.0 copy-start
  79.6 3.9 %copy.8 = f32[8,96,8,128]{3,2,1,0:T(8,128)} copy(f32[8,96,8,128]{3,2,1,0:T(8,128)} %bitcast.7) | data formatting | bytes 6291456
  83.5 0.0 copy-done
  83.5 1.7 %copy.9 = f32[8,96,8,128]{3,2,1,0:T(8,128)} copy(f32[8,96,8,128]{3,2,1,0:T(8,128)S(1)} %bitcast.6) | data formatting | bytes 6291456
Async XLA Ops:
  79.5 3.9 %copy-start = (f32[8,768,128]{2,1,0:T(8,128)S(1)}, f32[8,768,128]{2,1,0:T(8,128)}, u32[]{:S(2)}) copy-start(f32[8,768,128]{2,1,0:T(8,128)} %get-tuple-element.5) | copy-start | bytes 9437188

commit v2 on v1

--- a/solution.py
+++ b/solution.py
@@ -20,8 +20,8 @@
     return next(size for size in (2 * group, group) if columns % size == 0)
 
 
-def kernel(sizes, depth, field, flow_y, flow_x, flow_z, pot_out, end_out, u, end, pot, fy, fx, fz,
-           faces, halos, totals, totals_in, load_sem, store_sem, south_send, south_recv,
+def kernel(sizes, depth, field, flow_y, flow_x, flow_z, pot, end, u, fy, fx, fz,
+           faces, halos, totals, totals_in, load_sem, south_send, south_recv,
            east_send, east_recv, down_send, down_recv, tot_send, tot_recv):
     rows, cells, levels = field.shape
     columns = cells // depth
@@ -82,13 +82,19 @@
             send_sem=down_send.at[t, side, part], recv_sem=down_recv.at[t, side, part],
             device_id=beside("down", 1 if side == 0 else sizes["down"] - 1), device_id_type=MESH)
 
-    def total(hop, part):
-        start, count = blocks[part]
-        return pltpu.make_async_remote_copy(
-            src_ref=totals.at[pl.ds(start, count)],
-            dst_ref=totals_in.at[hop - 1, pl.ds(start, count)],
-            send_sem=tot_send.at[hop - 1, part], recv_sem=tot_recv.at[hop - 1, part],
+    def total(hop, piece, y0, count, x0, span):
+        cut = (pl.ds(y0, count), pl.ds(x0, span))
+        return pltpu.make_async_remote_copy(
+            src_ref=totals.at[cut], dst_ref=totals_in.at[(hop - 1, *cut)],
+            send_sem=tot_send.at[hop - 1, piece], recv_sem=tot_recv.at[hop - 1, piece],
             device_id=beside("down", hop), device_id_type=MESH)
+
+    def inner_total(hop):
+        return total(hop, 0, *blocks[0], 0, columns)
+
+    def rim_total(hop, side, c):
+        at = pl.multiple_of(c * width, group)
+        return total(hop, 1 + side * chunks + c, 0 if side == 0 else rows - 1, 1, at, width)
 
     place_in_block = lax.broadcasted_iota(jnp.int32, (depth, levels), 0)
     on_first, on_last = place_in_block == 0, place_in_block == depth - 1
@@ -139,26 +145,22 @@
 
         lax.fori_loop(0, count * groups, one, 0)
 
-    def finish(part):
-        for hop in range(1, sizes["down"]):
-            total(hop, part).wait_recv()
-
-        def one(y, x0):
-            for g in range(group):
-                own = pl.ds(pl.multiple_of((x0 + g) * depth, 8), depth)
-                value = pot[y, own, :]
-                for hop in range(1, sizes["down"]):
-                    below = jnp.broadcast_to(totals_in[hop - 1, y, pl.ds(x0 + g, 1), :], (depth, levels))
-                    value = value + jnp.where(places["down"] >= hop, below, 0.0)
-                pot[y, own, :] = value / (depth * sizes["down"])
-
-        over(*blocks[part], 0, columns, one)
-
-    def stores(part):
-        start, count = blocks[part]
-        cut = pl.ds(start, count)
-        return (pltpu.make_async_copy(end.at[cut], end_out.at[cut], store_sem.at[0, part]),
-                pltpu.make_async_copy(pot.at[cut], pot_out.at[cut], store_sem.at[1, part]))
+    def finish(y, x0):
+        for g in range(group):
+            own = pl.ds(pl.multiple_of((x0 + g) * depth, 8), depth)
+            value = pot[y, own, :]
+            for hop in range(1, sizes["down"]):
+                below = jnp.broadcast_to(totals_in[hop - 1, y, pl.ds(x0 + g, 1), :], (depth, levels))
+                value = value + jnp.where(places["down"] >= hop, below, 0.0)
+            pot[y, own, :] = value * (1.0 / (depth * sizes["down"]))
+
+    down_hops = range(1, sizes["down"])
+
+    def finish_rim(c):
+        for side in (0, 1):
+            for hop in down_hops:
+                rim_total(hop, side, c).wait_recv()
+            over(0 if side == 0 else rows - 1, 1, c * width, width, finish)
 
     def each_chunk(body):
         def one(c, carry):
@@ -193,11 +195,11 @@
                 east(t, side, 0).start()
                 down(t, side, 0).start()
         else:
-            stores(0)[0].start()
-            for hop in range(1, sizes["down"]):
-                total(hop, 0).start()
-            finish(0)
-            stores(0)[1].start()
+            for hop in down_hops:
+                inner_total(hop).start()
+            for hop in down_hops:
+                inner_total(hop).wait_recv()
+            over(*blocks[0], 0, columns, finish)
         for part in (1, 2):
             for side in (0, 1):
                 east(t - 1, side, part).wait_recv()
@@ -208,33 +210,41 @@
                 south(t - 1, side, c).wait_recv()
                 y = 0 if side == 0 else rows - 1
                 over(y, 1, c * width, width, functools.partial(march, t))
+                if t == STEPS:
+                    for hop in down_hops:
+                        rim_total(hop, side, c).start()
             if t < STEPS:
                 send_chunk(t, c)
+            else:
+                pl.when(c > 0)(lambda: finish_rim(c - 1))
 
         each_chunk(rim)
-        for part in (1, 2):
-            if t < STEPS:
+        if t < STEPS:
+            for part in (1, 2):
                 for side in (0, 1):
                     east(t, side, part).start()
                     down(t, side, part).start()
-            else:
-                stores(part)[0].start()
-                for hop in range(1, sizes["down"]):
-                    total(hop, part).start()
-    for part in (1, 2):
-        finish(part)
-        stores(part)[1].start()
+    finish_rim(chunks - 1)
     for t in range(STEPS):
         each_chunk(lambda c: [south(t, side, c).wait_send() for side in (0, 1)])
         for part in (0, 1, 2):
             for side in (0, 1):
                 east(t, side, part).wait_send()
                 down(t, side, part).wait_send()
-    for part in (0, 1, 2):
-        for hop in range(1, sizes["down"]):
-            total(hop, part).wait_send()
-        for store in stores(part):
-            store.wait()
+    for hop in down_hops:
+        inner_total(hop).wait_send()
+        each_chunk(lambda c: [rim_total(hop, side, c).wait_send() for side in (0, 1)])
+
+
+def write_out(*refs):
+    count = len(refs) // 2
+    sems = refs[-1]
+    pairs = zip(refs[:count], refs[count:-1])
+    copies = [pltpu.make_async_copy(src, dst, sems.at[i]) for i, (src, dst) in enumerate(pairs)]
+    for copy in copies:
+        copy.start()
+    for copy in copies:
+        copy.wait()
 
 
 def local(sizes, field_values, *flows):
@@ -248,27 +258,36 @@
     others = sizes["down"] - 1
     face = (rows, columns, levels)
     out = jax.ShapeDtypeStruct((rows, cells, levels), jnp.float32)
-    results = pl.pallas_call(
+    width_sems = (others, 1 + 2 * (columns // width))
+    held = pl.pallas_call(
         functools.partial(kernel, sizes, depth),
-        out_shape=(out, out),
+        out_shape=(block, block),
         in_specs=[pl.BlockSpec(memory_space=pl.ANY)] * 4,
-        out_specs=(pl.BlockSpec(memory_space=pl.ANY),) * 2,
+        out_specs=(pl.BlockSpec(memory_space=pltpu.VMEM),) * 2,
         scratch_shapes=[
             pltpu.VMEM((STEPS, rows + 2, cells + 2 * depth, levels), jnp.float32),
-            block, block, block, block, block,
+            block, block, block,
             pltpu.VMEM((STEPS, 2, *face), jnp.float32),
             pltpu.VMEM((STEPS, 2, *face), jnp.float32),
             pltpu.VMEM(face, jnp.float32),
             pltpu.VMEM((others, *face), jnp.float32),
-            dma((4,)), dma((2, 3)),
+            dma((4,)),
             dma(south_sems), dma(south_sems),
             dma(side_sems), dma(side_sems),
             dma(side_sems), dma(side_sems),
-            dma((others, 3)), dma((others, 3)),
+            dma(width_sems), dma(width_sems),
         ],
         compiler_params=pltpu.CompilerParams(
-            collective_id=0, has_side_effects=True, vmem_limit_bytes=60 * 1024 * 1024),
+            collective_id=0, has_side_effects=True, vmem_limit_bytes=48 * 1024 * 1024),
     )(*flat)
+    results = pl.pallas_call(
+        write_out,
+        out_shape=(out, out),
+        in_specs=[pl.BlockSpec(memory_space=pltpu.VMEM)] * 2,
+        out_specs=(pl.BlockSpec(memory_space=pltpu.HBM),) * 2,
+        scratch_shapes=[dma((2,))],
+        compiler_params=pltpu.CompilerParams(vmem_limit_bytes=8 * 1024 * 1024),
+    )(*held)
     return tuple(array.reshape(rows, columns, depth, levels) for array in results)
 
 

time: 85.3 us -> 81.6 us (0.957)
  local copies, waits for them, and re-layouts: 5.6 us -> 0 us
  Pallas kernels: 78.9 us -> 80.8 us
    unnamed x4 -> x0, local copies, waits for them, and re-layouts: 5.6 us -> none
    pallas_call x1 -> x2, Pallas kernels: 78.9 us -> 80.8 us  [the longest x1 78.1 us: local(): pl.pallas_call(functools.partial(kernel, sizes, depth), out_shape=(block,...]
where the time goes in v2:
time: 81.6 us; the launch traced here: 81.4 us
  Pallas kernels  80.8 us (99%)
    pallas_call x1, Pallas kernels, local(): pl.pallas_call(functools.partial(kernel, sizes, depth), out_shape=(block,...  78.1 us
    pallas_call x1, Pallas kernels, local(): pl.pallas_call(write_out, out_shape=(out, out), in_specs=[pl.BlockSpec(me...  2.72 us

profile of v2, /device:TPU:1, one launch (start us, length us, event | category | flops | bytes accessed | tf_op | source)
XLA Modules:
  0.0 81.4 jit_solution(8484018044370187823)
XLA Ops:
  0.6 78.1 %shard_map.59 = (f32[8,768,128]{2,1,0:T(8,128)S(1)}, f32[8,768,128]{2,1,0:T(8,128)S(1)}) custom-call(f32[8,768,128]{2,1,0:T(8,128)} %bitcast.6, f32[8,768,128]{2,1,0:T(8,128)} %bitcast.7, f32[8,768,128]{2,1,0:T(8,128)} %bitcast.8, f32[8,768,128]{2,1,0:T(8,128)} %bitcast.9), custom_call_target="tpu_custom_call" | custom-call | tf_op jit(solution)/shard_map/pallas_call | solution.py:262
  78.7 2.7 %shard_map.60 = (f32[8,768,128]{2,1,0:T(8,128)}, f32[8,768,128]{2,1,0:T(8,128)}) custom-call(f32[8,768,128]{2,1,0:T(8,128)S(1)} %get-tuple-element.6.refs_0_, f32[8,768,128]{2,1,0:T(8,128)S(1)} %get-tuple-element.7.refs_1_), custom_call_target="tpu_custom_call" | custom-call | tf_op jit(solution)/shard_map/pallas_call | solution.py:283

commit v3 on v2

--- a/solution.py
+++ b/solution.py
@@ -17,7 +17,7 @@
 
 
 def chunk_of(columns, group):
-    return next(size for size in (2 * group, group) if columns % size == 0)
+    return next(size for size in (4 * group, 2 * group, group) if columns % size == 0)
 
 
 def kernel(sizes, depth, field, flow_y, flow_x, flow_z, pot, end, u, fy, fx, fz,
@@ -40,21 +40,23 @@
         pl.semaphore_signal(barrier, inc=1, device_id=beside(axis, hop), device_id_type=MESH)
 
     flows = ((flow_y, fy), (flow_x, fx), (flow_z, fz))
-    loads = [pltpu.make_async_copy(field, u.at[0, pl.ds(1, rows), pl.ds(depth, cells), :], load_sem.at[0])]
-    loads += [pltpu.make_async_copy(src, dst, load_sem.at[1 + i]) for i, (src, dst) in enumerate(flows)]
-    for load in loads:
+    loads = [
+        pltpu.make_async_copy(
+            field.at[pl.ds(start, count)], u.at[0, pl.ds(start + 1, count), pl.ds(depth, cells), :],
+            load_sem.at[i])
+        for i, (start, count) in enumerate(((0, 1), (rows - 1, 1), (1, rows - 2)))]
+    loads += [pltpu.make_async_copy(src, dst, load_sem.at[3 + i]) for i, (src, dst) in enumerate(flows)]
+    for load in loads[:2]:
         load.start()
+    for load in loads[:2]:
+        load.wait()
     pl.semaphore_wait(barrier, len(hops))
 
     def south(t, side, c):
         row = rows - 1 if side == 0 else 0
         at = pl.multiple_of(c * width * depth, 8)
-        if t == 0:
-            src = field.at[row, pl.ds(at, width * depth), :]
-        else:
-            src = u.at[t, row + 1, pl.ds(at + depth, width * depth), :]
         return pltpu.make_async_remote_copy(
-            src_ref=src,
+            src_ref=u.at[t, row + 1, pl.ds(at + depth, width * depth), :],
             dst_ref=u.at[t, 0 if side == 0 else rows + 1, pl.ds(at + depth, width * depth), :],
             send_sem=south_send.at[t, side, c], recv_sem=south_recv.at[t, side, c],
             device_id=beside("south", 1 if side == 0 else sizes["south"] - 1), device_id_type=MESH)
@@ -174,15 +176,17 @@
             south(t, side, c).start()
 
     each_chunk(lambda c: send_chunk(0, c))
+    for load in loads[2:]:
+        load.start()
     for part in (0, 1, 2):
         for side in (0, 1):
             east(0, side, part).start()
-    loads[0].wait()
+    loads[2].wait()
     for part in (0, 1, 2):
         over(*blocks[part], 0, columns, functools.partial(take_faces, 0))
         for side in (0, 1):
             down(0, side, part).start()
-    for load in loads[1:]:
+    for load in loads[3:]:
         load.wait()
 
     for t in range(1, STEPS + 1):
@@ -240,7 +244,9 @@
     count = len(refs) // 2
     sems = refs[-1]
     pairs = zip(refs[:count], refs[count:-1])
-    copies = [pltpu.make_async_copy(src, dst, sems.at[i]) for i, (src, dst) in enumerate(pairs)]
+    copies = [
+        pltpu.make_async_copy(src.at[row], dst.at[row], sems.at[i, row])
+        for i, (src, dst) in enumerate(pairs) for row in range(src.shape[0])]
     for copy in copies:
         copy.start()
     for copy in copies:
@@ -271,7 +277,7 @@
             pltpu.VMEM((STEPS, 2, *face), jnp.float32),
             pltpu.VMEM(face, jnp.float32),
             pltpu.VMEM((others, *face), jnp.float32),
-            dma((4,)),
+            dma((6,)),
             dma(south_sems), dma(south_sems),
             dma(side_sems), dma(side_sems),
             dma(side_sems), dma(side_sems),
@@ -285,7 +291,7 @@
         out_shape=(out, out),
         in_specs=[pl.BlockSpec(memory_space=pltpu.VMEM)] * 2,
         out_specs=(pl.BlockSpec(memory_space=pltpu.HBM),) * 2,
-        scratch_shapes=[dma((2,))],
+        scratch_shapes=[dma((2, rows))],
         compiler_params=pltpu.CompilerParams(vmem_limit_bytes=8 * 1024 * 1024),
     )(*held)
     return tuple(array.reshape(rows, columns, depth, levels) for array in results)

time: 81.6 us -> 80.6 us (0.988)
  Pallas kernels: 80.8 us -> 79.8 us
    pallas_call x1, Pallas kernels: 78.1 us -> 77 us  [local(): pl.pallas_call(functools.partial(kernel, sizes, depth), out_shape=(block,...]
where the time goes in v3:
time: 80.6 us; the launch traced here: 80.4 us
  Pallas kernels  79.8 us (99%)
    pallas_call x1, Pallas kernels, local(): pl.pallas_call(functools.partial(kernel, sizes, depth), out_shape=(block,...  77 us
    pallas_call x1, Pallas kernels, local(): pl.pallas_call(write_out, out_shape=(out, out), in_specs=[pl.BlockSpec(me...  2.78 us

profile of v3, /device:TPU:1, one launch (start us, length us, event | category | flops | bytes accessed | tf_op | source)
XLA Modules:
  0.0 80.4 jit_solution(1088942959519297607)
XLA Ops:
  0.6 77.0 %shard_map.59 = (f32[8,768,128]{2,1,0:T(8,128)S(1)}, f32[8,768,128]{2,1,0:T(8,128)S(1)}) custom-call(f32[8,768,128]{2,1,0:T(8,128)} %bitcast.6, f32[8,768,128]{2,1,0:T(8,128)} %bitcast.7, f32[8,768,128]{2,1,0:T(8,128)} %bitcast.8, f32[8,768,128]{2,1,0:T(8,128)} %bitcast.9), custom_call_target="tpu_custom_call" | custom-call | tf_op jit(solution)/shard_map/pallas_call | solution.py:268
  77.6 2.8 %shard_map.60 = (f32[8,768,128]{2,1,0:T(8,128)}, f32[8,768,128]{2,1,0:T(8,128)}) custom-call(f32[8,768,128]{2,1,0:T(8,128)S(1)} %get-tuple-element.6.refs_0_, f32[8,768,128]{2,1,0:T(8,128)S(1)} %get-tuple-element.7.refs_1_), custom_call_target="tpu_custom_call" | custom-call | tf_op jit(solution)/shard_map/pallas_call | solution.py:289
